TPU v7x, 512 devices: a whole 4x8x8 slice. The times are simulated.
512 devices in a mesh: pb: 8 (over x, core), ka: 64 (over z, y).
Axes of the slice: x: 4, y: 8, z: 8, core: 2. Of those that a mesh axis runs over, the one named last changes fastest.
Arguments:
- coupling: bfloat16 [8, 64, 128, 32, 384], P('pb', 'ka'), may hold values from -0.796875 to 0.796875
- phonon_occ: float32 [8, 64, 128, 12], P('pb', 'ka'), may hold values from 0.1 to 1
- band_window: int32 [8, 64, 128, 32], P('pb', 'ka'), may hold values 0 or 1
- pair_count: int32 [8, 64, 64], P('pb', 'ka'), may hold values from 0 to 2, as said below
- k_target: int32 [8, 64, 128], P('pb', 'ka'), may hold values from 0 to 127
- kq_source: int32 [8, 64, 128], P('pb', 'ka'), may hold values from 0 to 127
- velocity: float32 [3, 32, 8192], P(None, None, 'ka'), may hold values from -6 to 6
- lifetime: float32 [32, 8192], P(None, 'ka'), may hold values from 0.5 to 2
Outputs:
- deviation: float32 [3, 32, 8192], P(None, None, 'ka')
Inputs may be any that keep to these rules, and one draw needn't show every extreme that they name: pair_count[p, a, d] is the number of live tile slots among slots d * 2 to d * 2 + 1 of device (p, a); in every q-group p some owner d receives 2 live tiles from every source.
All inputs are finite; a program needn't handle non-finite values. No bound on the sum of `band_window` on one device may be relied on, other than what follows from the above.
Results may differ from a plain program's by a relative error of at most 0.012.
Values may be sent and summed in bfloat16 or wider, within the bound.
No kernel may reach another device: no remote copies, remote signals or barrier semaphores. Data moves between devices by JAX's collectives and lax.ppermute only.
A program may use at most 64 MiB of HBM per device.

v0:
```python
import jax
import jax.numpy as jnp
from jax import lax
from jax.experimental import pallas as pl
from jax.experimental.pallas import tpu as pltpu
from jax.sharding import PartitionSpec as P


MODES = 12
TILE_SLOTS = 2
BANDS = 32
ROWS = 3 * BANDS
TILES = 128
LANES = BANDS * MODES
CHUNKS = (16, 32, 40, 40)
PB = ("x", "core")
WIDE = BANDS * BANDS
F32 = jnp.float32
BF16 = jnp.bfloat16


def iota(shape, axis):
    return lax.broadcasted_iota(jnp.int32, shape, axis)


def band_terms(weight, base, pairs, half_ref, term_ref, slot):
    for q in range(8):
        total = None
        for m, pair in enumerate(pairs):
            term = weight[pl.ds(q * TILES + m * 8, 8), :].astype(F32) * pair
            total = term if total is None else total + term
        half_ref[pl.ds(base + q * 8, 8), :] = total
    for j in range(4):
        term_ref[pl.ds(slot * BANDS + j * 8, 8), :] = (
            half_ref[pl.ds(base + j, 8, stride=8), :] + half_ref[pl.ds(base + j + 4, 8, stride=8), :]
        )


def band_pairs(chosen_ref, slot):
    first = iota((8, TILES), 0) < 4
    pairs = []
    for m in range(0, BANDS, 2):
        row = slot * BANDS + m
        low = jnp.broadcast_to(chosen_ref[pl.ds(row, 1), :], (8, TILES))
        high = jnp.broadcast_to(chosen_ref[pl.ds(row + 1, 1), :], (8, TILES))
        pairs.append(jnp.where(first, low, high))
    return pairs


def onehot(equal):
    return equal.astype(F32).astype(BF16)


def weight_kernel(
    coupling, occ, window, count, source, target, velocity, lifetime,
    wide_ref, out_ref, state_ref,
    weight_ref, index_ref, tiles, flat, occ_wide, occ_pad, window_ref, count_ref, mask_ref, chosen_ref, half_ref, term_ref, sems, small_sems,
):
    small = []
    for place, (origin, into) in enumerate((
        *((occ.at[v], occ_pad.at[pl.ds(v, 1)]) for v in range(MODES)),
        (count, count_ref),
        (window, window_ref),
        (velocity, state_ref.at[pl.ds(0, ROWS)]),
        (lifetime, state_ref.at[pl.ds(ROWS, BANDS)]),
        (source, index_ref.at[pl.ds(0, 1)]),
        (target, index_ref.at[pl.ds(1, 1)]),
    )):
        small.append(pltpu.make_async_copy(origin, into, small_sems.at[place]))
    begin = [sum(CHUNKS[:c]) for c in range(len(CHUNKS))]
    copies = []
    for c, size in enumerate(CHUNKS):
        part = pl.ds(begin[c], size)
        copies.append(pltpu.make_async_copy(coupling.at[part], tiles.at[part], sems.at[c]))
        copies[-1].start()
        if c == 0:
            for copy in small[:MODES]:
                copy.start()
    for copy in small[MODES:]:
        copy.start()
    spread = (iota((16, LANES), 1) % MODES == iota((16, LANES), 0)).astype(F32).astype(BF16)
    gather = (iota((LANES, TILES), 0) // MODES == iota((LANES, TILES), 1) // 4).astype(F32).astype(BF16)
    group = iota((1, TILES), 1) % 4
    for copy in small[:MODES]:
        copy.wait()
    valid = iota((16, TILES), 0) < MODES
    occ_rows = jnp.where(valid, occ_pad[...], 0.0).T.astype(BF16)
    occ_wide[...] = jnp.dot(occ_rows, spread, preferred_element_type=F32)
    for c, size in enumerate(CHUNKS):
        copies[c].wait()
        rows = []
        for t in range(begin[c], begin[c] + size):
            tile = tiles[t]
            wide = jnp.broadcast_to(occ_wide[pl.ds(t, 1), :], (BANDS, LANES)).astype(BF16)
            rows.append(tile * tile * wide)
        summed = jnp.dot(jnp.concatenate(rows, axis=0), gather, preferred_element_type=F32)
        for t in range(size):
            merged = summed[t * BANDS : t * BANDS + 8, :]
            for j in range(1, 4):
                row = t * BANDS + j * 8
                merged = jnp.where(group == j, summed[row : row + 8, :], merged)
            flat[pl.ds((begin[c] + t) * 8, 8), :] = merged
    for copy in small[MODES:]:
        copy.wait()
    count = count_ref[...].astype(F32).astype(BF16)
    owner = (iota((64, TILES), 1) // TILE_SLOTS == iota((64, TILES), 0)).astype(F32).astype(BF16)
    live = jnp.dot(jnp.broadcast_to(count, (8, 64)), owner, preferred_element_type=F32)
    slot = (iota((8, TILES), 1) % TILE_SLOTS).astype(F32)
    live = (slot < live).astype(F32)
    mask = window_ref[...].astype(F32) * live[0:1, :]
    mask_ref[pl.ds(0, BANDS), :] = mask
    mask_ref[pl.ds(BANDS, BANDS), :] = mask
    for q in range(8):
        turned = flat[pl.ds(q, TILES, stride=8), :].T
        rows = mask_ref[pl.ds(q, 8, stride=8), :]
        for m in range(16):
            weight_ref[pl.ds(q * TILES + m * 8, 8), :] = turned[m * 8 : m * 8 + 8, :] * rows
    source_row = jnp.broadcast_to(index_ref[0:1, :], (16, TILES))
    wide_ref[pl.ds(0, WIDE), :] = weight_ref[...].astype(BF16)
    wide_ref[pl.ds(WIDE, 16), :] = source_row.astype(F32).astype(BF16)
    lifetime_now = state_ref[pl.ds(ROWS, BANDS), :]
    deviation = jnp.concatenate(
        [lifetime_now * state_ref[pl.ds(i * BANDS, BANDS), :] for i in range(3)], axis=0
    )
    picks = onehot(iota((TILES, TILES), 0) == index_ref[0:1, :])
    chosen_ref[...] = jnp.dot(deviation.astype(BF16), picks, preferred_element_type=F32)
    for i in range(3):
        band_terms(weight_ref, i * 64, band_pairs(chosen_ref, i), half_ref, term_ref, i)
    target = index_ref[1:2, :].astype(F32)
    term_ref[pl.ds(ROWS, BANDS), :] = jnp.where(iota((BANDS, TILES), 0) == 0, target, 0.0)
    out_ref[...] = term_ref[...].T.astype(BF16)


def receive_kernel(terms_ref, out_ref):
    terms = terms_ref[...].astype(F32)
    target = terms[:, ROWS : ROWS + 1].astype(jnp.int32)
    turned = terms.T
    places = onehot(iota((TILES, TILES), 1) == target)
    total = jnp.dot(turned[:ROWS, :].astype(BF16), places, preferred_element_type=F32)
    message = jnp.concatenate([total, turned[ROWS : ROWS + 8, :]], axis=0).astype(BF16)
    for p in range(out_ref.shape[0]):
        out_ref[p] = message


def direction_terms(deviation, weights, chosen_ref, half_ref, term_ref, out_ref):
    picks = []
    for weight in weights:
        source_row = weight[pl.ds(WIDE, 16), :].astype(F32)[0:1, :].astype(jnp.int32)
        picks.append(onehot(iota((TILES, TILES), 0) == source_row))
    chosen = jnp.dot(deviation.astype(BF16), jnp.concatenate(picks, axis=1), preferred_element_type=F32)
    for g, weight in enumerate(weights):
        chosen_ref[pl.ds(g * BANDS, BANDS), :] = chosen[:, g * TILES : (g + 1) * TILES]
    for g, weight in enumerate(weights):
        band_terms(weight, g * 64, band_pairs(chosen_ref, g), half_ref, term_ref, g)
    message = term_ref[...].T.astype(BF16)
    for core in range(out_ref.shape[0]):
        out_ref[core] = message


def own_direction():
    return lax.axis_index("x") % 3


def next_direction(state_ref, scattering):
    rows = pl.ds(pl.multiple_of(own_direction() * BANDS, BANDS), BANDS)
    return state_ref[pl.ds(ROWS, BANDS), :] * (state_ref[rows, :] + scattering)


def first_kernel(parts_ref, state_ref, w0, w1, w2, w3, out_ref, target_ref, chosen_ref, half_ref, term_ref):
    rows = pl.ds(pl.multiple_of(own_direction() * BANDS, BANDS), BANDS)
    total = parts_ref[0, rows, :].astype(F32)
    for p in range(1, parts_ref.shape[0]):
        total = total + parts_ref[p, rows, :].astype(F32)
    for g in range(4):
        for core in range(2):
            peer = 2 * jnp.bitwise_xor(lax.axis_index("x"), g) + core
            row = parts_ref[peer, pl.ds(ROWS, 8), :].astype(F32)[0:1, :]
            target_ref[pl.ds(2 * g + core, 1), :] = row
    deviation = next_direction(state_ref, total)
    direction_terms(deviation, (w0, w1, w2, w3), chosen_ref, half_ref, term_ref, out_ref)


def direction_sum(terms_ref, target_ref, cores):
    turned = terms_ref[...].astype(F32).T.astype(BF16)
    left, right = [], []
    for g in range(4):
        left.append(turned[g * BANDS : (g + 1) * BANDS, :])
        for core in cores:
            target = target_ref[pl.ds(2 * g + core, 1), :].astype(jnp.int32)
            right.append(onehot(iota((TILES, TILES), 0) == target))
    return lax.dot_general(
        jnp.concatenate(left, axis=1), jnp.concatenate(right, axis=1), (((1,), (1,)), ((), ())),
        preferred_element_type=F32,
    )


def step_kernel(terms_ref, target_ref, state_ref, w0, w1, w2, w3, out_ref, chosen_ref, half_ref, term_ref):
    deviation = next_direction(state_ref, direction_sum(terms_ref, target_ref, (0, 1)))
    direction_terms(deviation, (w0, w1, w2, w3), chosen_ref, half_ref, term_ref, out_ref)


def last_kernel(terms_ref, target_ref, out_ref):
    total = direction_sum(terms_ref, target_ref, (lax.axis_index("core"),)).astype(BF16)
    for p in range(out_ref.shape[0]):
        out_ref[p] = total


def final_kernel(parts_ref, state_ref, out_ref):
    for i in range(3):
        total = parts_ref[2 * i].astype(F32) + parts_ref[2 * i + 1].astype(F32)
        rows = pl.ds(i * BANDS, BANDS)
        out_ref[rows, :] = state_ref[pl.ds(ROWS, BANDS), :] * (state_ref[rows, :] + total)


VMEM = pl.BlockSpec(memory_space=pltpu.VMEM)


def call(body, ins, outs, scratch=(), limit=4 << 20, flops=1000000):
    return pl.pallas_call(
        body,
        in_specs=ins,
        out_specs=[VMEM] * len(outs),
        out_shape=[jax.ShapeDtypeStruct(s, d) for s, d in outs],
        scratch_shapes=list(scratch),
        compiler_params=pltpu.CompilerParams(vmem_limit_bytes=limit),
        cost_estimate=pl.CostEstimate(flops=flops, bytes_accessed=1 << 20, transcendentals=0),
    )


def over_owners(terms, axes):
    return lax.all_to_all(
        terms.reshape(-1, TILE_SLOTS, TILES), axes, split_axis=0, concat_axis=0, tiled=True
    ).reshape(-1, TILES)


def shards(coupling, phonon_occ, band_window, pair_count, k_target, kq_source, velocity, lifetime):
    groups = lax.axis_size("x") * lax.axis_size("core")
    small = [
        pltpu.VMEM((TILES, TILES), F32), pltpu.VMEM((4 * 64, TILES), F32), pltpu.VMEM((TILES, TILES), F32)
    ]
    wide, terms, state = call(
        weight_kernel, [pl.BlockSpec(memory_space=pltpu.HBM)] * 8,
        [((WIDE + 16, TILES), BF16), ((TILES, TILES), BF16), ((TILES, TILES), F32)],
        [
            pltpu.VMEM((WIDE, TILES), F32),
            pltpu.VMEM((8, TILES), jnp.int32),
            pltpu.VMEM((TILES, BANDS, LANES), BF16),
            pltpu.VMEM((TILES * 8, TILES), F32),
            pltpu.VMEM((TILES, LANES), F32),
            pltpu.VMEM((16, TILES), F32),
            pltpu.VMEM((BANDS, TILES), jnp.int32),
            pltpu.VMEM((1, 64), jnp.int32),
            pltpu.VMEM((2 * BANDS, TILES), F32),
            pltpu.VMEM((ROWS, TILES), F32), *small[1:],
            pltpu.SemaphoreType.DMA((len(CHUNKS),)),
            pltpu.SemaphoreType.DMA((MODES + 6,)),
        ],
        limit=16 << 20,
    )(*(pltpu.with_memory_space_constraint(x, pltpu.HBM) for x in (
        coupling[0, 0], phonon_occ.transpose(0, 3, 1, 2).reshape(MODES, 1, TILES), band_window[0, 0].T, pair_count[0],
        kq_source.reshape(1, TILES), k_target.reshape(1, TILES), velocity.reshape(ROWS, TILES), lifetime,
    )))
    arrived = over_owners(terms, "ka")
    weights = [wide]
    for flip in (2, 4, 6):
        weights.append(lax.ppermute(wide, PB, [(p, p ^ flip) for p in range(groups) if p ^ flip < 6]))
    (copies,) = call(receive_kernel, [VMEM], [((groups, ROWS + 8, TILES), BF16)])(arrived)
    parts = lax.all_to_all(copies, PB, split_axis=0, concat_axis=0, tiled=True)
    terms, targets = call(
        first_kernel, [VMEM] * 6, [((2, TILES, TILES), BF16), ((8, TILES), F32)], small
    )(parts, state, *weights)
    for copied in (2, 1):
        arrived = over_owners(terms, ("core", "ka"))
        (terms,) = call(step_kernel, [VMEM] * 7, [((copied, TILES, TILES), BF16)], small)(
            arrived, targets, state, *weights
        )
    arrived = over_owners(terms, "ka")
    (copies,) = call(last_kernel, [VMEM] * 2, [((groups, BANDS, TILES), BF16)])(arrived, targets)
    parts = lax.all_to_all(copies, PB, split_axis=0, concat_axis=0, tiled=True)
    (deviation,) = call(final_kernel, [VMEM] * 2, [((ROWS, TILES), F32)])(parts, state)
    return deviation.reshape(3, BANDS, TILES)


def solution(mesh):
    fine = jax.sharding.Mesh(mesh.devices.reshape(4, 2, -1), (*PB, "ka"))
    placed = (
        P(PB, "ka", None, None, None),
        P(PB, "ka", None, None),
        P(PB, "ka", None, None),
        P(PB, "ka", None),
        P(PB, "ka", None),
        P(PB, "ka", None),
        P(None, None, "ka"),
        P(None, "ka"),
    )
    return jax.shard_map(
        shards, mesh=fine, in_specs=placed, out_specs=P(None, None, "ka"), check_vma=False
    )
```

profile of v0, /device:TPU:1, one launch (start us, length us, event | category | flops | bytes accessed | tf_op | source)
XLA Modules:
  0.0 113.8 jit_solution(10378774544916558596)
XLA Ops:
  0.0 3.5 %shard_map.82 = (bf16[1040,128]{1,0:T(8,128)(2,1)S(1)}, bf16[128,128]{1,0:T(8,128)(2,1)S(1)}, f32[128,128]{1,0:T(8,128)S(1)}) custom-call(bf16[128,32,384]{2,1,0:T(8,128)(2,1)} %bitcast.28, f32[12,1,128]{2,1,0:T(1,128)} %bitcast.31, s32[32,128]{1,0:T(8,128)} %bitcast.30, s32[1,64]{1,0:T(1,128)} %bitcast.32, s32[1,128]{1,0:T(1,128)} %bitcast.33, ...), custom_call_target="tpu_custom_call" | custom-call | flops 1000000 | bytes 1048576 | tf_op jit(solution)/shard_map/pallas_call | solution.py:241
  3.5 1.3 %collective-permute-start.2 = (bf16[1040,128]{1,0:T(8,128)(2,1)S(1)}, bf16[1040,128]{1,0:T(8,128)(2,1)S(1)}, u32[]{:S(2)}, u32[]{:S(2)}) collective-permute-start(bf16[1040,128]{1,0:T(8,128)(2,1)S(1)} %get-tuple-element.12.w0), channel_id=1, source_target_pairs={{128,256},{192,320},{256,128},{320,192},{384,0},{448,64},{129,257}... | collective-permute-start | bytes 798728 | tf_op jit(solution)/shard_map/ppermute | solution.py:266
  4.8 6.3 %collective-permute-start.1 = (bf16[1040,128]{1,0:T(8,128)(2,1)S(1)}, bf16[1040,128]{1,0:T(8,128)(2,1)S(1)}, u32[]{:S(2)}, u32[]{:S(2)}) collective-permute-start(bf16[1040,128]{1,0:T(8,128)(2,1)S(1)} %get-tuple-element.12.w0), channel_id=1, source_target_pairs={{0,256},{64,320},{256,0},{320,64},{384,128},{448,192},{1,257},{65,... | collective-permute-start | bytes 798728 | tf_op jit(solution)/shard_map/ppermute | solution.py:266
  11.1 1.9 %collective-permute-start = (bf16[1040,128]{1,0:T(8,128)(2,1)S(1)}, bf16[1040,128]{1,0:T(8,128)(2,1)S(1)}, u32[]{:S(2)}, u32[]{:S(2)}) collective-permute-start(bf16[1040,128]{1,0:T(8,128)(2,1)S(1)} %get-tuple-element.12.w0), channel_id=1, source_target_pairs={{0,128},{64,192},{128,0},{192,64},{384,256},{448,320},{1,129},{65,... | collective-permute-start | bytes 798728 | tf_op jit(solution)/shard_map/ppermute | solution.py:266
  13.0 27.0 %all_to_all.30 = bf16[64,2,128]{2,1,0:T(2,128)(2,1)S(1)} all-to-all(bf16[64,2,128]{2,1,0:T(2,128)(2,1)S(1)} %bitcast.27), channel_id=1, replica_groups=mesh['x'=4,'core'=2,'ka'=64] {'ka'}, dimensions={0} | all-to-all | bytes 65536 | tf_op jit(solution)/shard_map/all_to_all | solution.py:231
  40.0 0.2 shard_map.83
  40.3 11.8 %all_to_all.31.parts_ref = bf16[8,104,128]{2,1,0:T(8,128)(2,1)S(1)} all-to-all(bf16[8,104,128]{2,1,0:T(8,128)(2,1)S(1)} %shard_map.83), channel_id=1, replica_groups=mesh['x'=4,'core'=2,'ka'=64] {'x','core'}, dimensions={0} | all-to-all | bytes 425984 | tf_op jit(solution)/shard_map/all_to_all | solution.py:268
  52.0 0.0 collective-permute-done.2.w3
  52.0 0.0 collective-permute-done.1.w2
  52.0 0.0 collective-permute-done.w1
  52.0 0.5 shard_map.84
  52.5 17.8 %all_to_all.32 = bf16[128,2,128]{2,1,0:T(2,128)(2,1)S(1)} all-to-all(bf16[128,2,128]{2,1,0:T(2,128)(2,1)S(1)} %bitcast.26), channel_id=1, replica_groups=mesh['x'=4,'core'=2,'ka'=64] {'core','ka'}, dimensions={0} | all-to-all | bytes 131072 | tf_op jit(solution)/shard_map/all_to_all | solution.py:231
  70.3 0.7 shard_map.85
  71.0 17.6 %all_to_all.33 = bf16[128,2,128]{2,1,0:T(2,128)(2,1)S(1)} all-to-all(bf16[128,2,128]{2,1,0:T(2,128)(2,1)S(1)} %bitcast.22), channel_id=1, replica_groups=mesh['x'=4,'core'=2,'ka'=64] {'core','ka'}, dimensions={0} | all-to-all | bytes 131072 | tf_op jit(solution)/shard_map/all_to_all | solution.py:231
  88.6 0.7 shard_map.86
  89.2 14.7 %all_to_all.34 = bf16[64,2,128]{2,1,0:T(2,128)(2,1)S(1)} all-to-all(bf16[64,2,128]{2,1,0:T(2,128)(2,1)S(1)} %bitcast.23), channel_id=1, replica_groups=mesh['x'=4,'core'=2,'ka'=64] {'ka'}, dimensions={0} | all-to-all | bytes 65536 | tf_op jit(solution)/shard_map/all_to_all | solution.py:231
  103.9 0.2 shard_map.87
  104.1 9.1 %all_to_all.35.parts_ref = bf16[8,32,128]{2,1,0:T(8,128)(2,1)S(1)} all-to-all(bf16[8,32,128]{2,1,0:T(8,128)(2,1)S(1)} %shard_map.87), channel_id=1, replica_groups=mesh['x'=4,'core'=2,'ka'=64] {'x','core'}, dimensions={0} | all-to-all | bytes 131072 | tf_op jit(solution)/shard_map/all_to_all | solution.py:279
  113.2 0.6 shard_map.88
Async XLA Ops:
  3.5 48.6 %collective-permute-start.2 = (bf16[1040,128]{1,0:T(8,128)(2,1)S(1)}, bf16[1040,128]{1,0:T(8,128)(2,1)S(1)}, u32[]{:S(2)}, u32[]{:S(2)}) collective-permute-start(bf16[1040,128]{1,0:T(8,128)(2,1)S(1)} %get-tuple-element.12.w0), channel_id=1, source_target_pairs={{128,256},{192,320},{256,128},{320,192},{384,0},{448,64},{129,257}... | collective-permute-start | bytes 798728 | tf_op jit(solution)/shard_map/ppermute | solution.py:266
  4.8 47.3 %collective-permute-start.1 = (bf16[1040,128]{1,0:T(8,128)(2,1)S(1)}, bf16[1040,128]{1,0:T(8,128)(2,1)S(1)}, u32[]{:S(2)}, u32[]{:S(2)}) collective-permute-start(bf16[1040,128]{1,0:T(8,128)(2,1)S(1)} %get-tuple-element.12.w0), channel_id=1, source_target_pairs={{0,256},{64,320},{256,0},{320,64},{384,128},{448,192},{1,257},{65,... | collective-permute-start | bytes 798728 | tf_op jit(solution)/shard_map/ppermute | solution.py:266
  11.1 40.9 %collective-permute-start = (bf16[1040,128]{1,0:T(8,128)(2,1)S(1)}, bf16[1040,128]{1,0:T(8,128)(2,1)S(1)}, u32[]{:S(2)}, u32[]{:S(2)}) collective-permute-start(bf16[1040,128]{1,0:T(8,128)(2,1)S(1)} %get-tuple-element.12.w0), channel_id=1, source_target_pairs={{0,128},{64,192},{128,0},{192,64},{384,256},{448,320},{1,129},{65,... | collective-permute-start | bytes 798728 | tf_op jit(solution)/shard_map/ppermute | solution.py:266
where the time goes:
time: 114 us
  blocking collectives  97.9 us (86%)
  starting transfers between devices  9.55 us (8%)
  Pallas kernels  6.31 us (6%)
    all_to_all x4, blocking collectives, over_owners(): lax.all_to_all(terms.reshape(-1, TILE_SLOTS, TILES), axes, split_axis=0,...  77 us
    all_to_all x2, blocking collectives, shards(): parts = lax.all_to_all(copies, PB, split_axis=0, concat_axis=0, tiled=True)  20.9 us
    ppermute x3, starting transfers between devices, shards(): lax.ppermute(wide, PB, [(p, p ^ flip) for p in range(groups) if p ^ flip...  9.55 us
    pallas_call x1, Pallas kernels, shards(): call(weight_kernel, [pl.BlockSpec(memory_space=pltpu.HBM)] * 8, [((WIDE +...  3.46 us
  transfers between devices with their start and end apart: 3, of which 0 were waited for; matrix products, arithmetic and copies ran while one was open for 0% of the time, Pallas kernels for 0%

commit v1 on v0

--- a/solution.py
+++ b/solution.py
@@ -12,7 +12,7 @@
 ROWS = 3 * BANDS
 TILES = 128
 LANES = BANDS * MODES
-CHUNKS = (16, 32, 40, 40)
+CHUNKS = (24, 48, 56)
 PB = ("x", "core")
 WIDE = BANDS * BANDS
 F32 = jnp.float32
@@ -137,9 +137,13 @@
     turned = terms.T
     places = onehot(iota((TILES, TILES), 1) == target)
     total = jnp.dot(turned[:ROWS, :].astype(BF16), places, preferred_element_type=F32)
-    message = jnp.concatenate([total, turned[ROWS : ROWS + 8, :]], axis=0).astype(BF16)
+    targets = turned[ROWS : ROWS + 8, :]
+    messages = [
+        jnp.concatenate([total[i * BANDS : (i + 1) * BANDS, :], targets], axis=0).astype(BF16)
+        for i in range(3)
+    ]
     for p in range(out_ref.shape[0]):
-        out_ref[p] = message
+        out_ref[p] = messages[p // 2 % 3]
 
 
 def direction_terms(deviation, weights, chosen_ref, half_ref, term_ref, out_ref):
@@ -167,14 +171,13 @@
 
 
 def first_kernel(parts_ref, state_ref, w0, w1, w2, w3, out_ref, target_ref, chosen_ref, half_ref, term_ref):
-    rows = pl.ds(pl.multiple_of(own_direction() * BANDS, BANDS), BANDS)
-    total = parts_ref[0, rows, :].astype(F32)
+    total = parts_ref[0, pl.ds(0, BANDS), :].astype(F32)
     for p in range(1, parts_ref.shape[0]):
-        total = total + parts_ref[p, rows, :].astype(F32)
+        total = total + parts_ref[p, pl.ds(0, BANDS), :].astype(F32)
     for g in range(4):
         for core in range(2):
             peer = 2 * jnp.bitwise_xor(lax.axis_index("x"), g) + core
-            row = parts_ref[peer, pl.ds(ROWS, 8), :].astype(F32)[0:1, :]
+            row = parts_ref[peer, pl.ds(BANDS, 8), :].astype(F32)[0:1, :]
             target_ref[pl.ds(2 * g + core, 1), :] = row
     deviation = next_direction(state_ref, total)
     direction_terms(deviation, (w0, w1, w2, w3), chosen_ref, half_ref, term_ref, out_ref)
@@ -264,7 +267,7 @@
     weights = [wide]
     for flip in (2, 4, 6):
         weights.append(lax.ppermute(wide, PB, [(p, p ^ flip) for p in range(groups) if p ^ flip < 6]))
-    (copies,) = call(receive_kernel, [VMEM], [((groups, ROWS + 8, TILES), BF16)])(arrived)
+    (copies,) = call(receive_kernel, [VMEM], [((groups, BANDS + 8, TILES), BF16)])(arrived)
     parts = lax.all_to_all(copies, PB, split_axis=0, concat_axis=0, tiled=True)
     terms, targets = call(
         first_kernel, [VMEM] * 6, [((2, TILES, TILES), BF16), ((8, TILES), F32)], small

time: 114 us -> 113 us (level)
  blocking collectives: 97.9 us -> 96.6 us
where the time goes in v1:
time: 113 us
  blocking collectives  96.6 us (85%)
  starting transfers between devices  9.55 us (8%)
  Pallas kernels  6.33 us (6%)
    all_to_all x4, blocking collectives, over_owners(): lax.all_to_all(terms.reshape(-1, TILE_SLOTS, TILES), axes, split_axis=0,...  76.9 us
    all_to_all x2, blocking collectives, shards(): parts = lax.all_to_all(copies, PB, split_axis=0, concat_axis=0, tiled=True)  19.8 us
    ppermute x3, starting transfers between devices, shards(): lax.ppermute(wide, PB, [(p, p ^ flip) for p in range(groups) if p ^ flip...  9.55 us
    pallas_call x1, Pallas kernels, shards(): call(weight_kernel, [pl.BlockSpec(memory_space=pltpu.HBM)] * 8, [((WIDE +...  3.48 us
  transfers between devices with their start and end apart: 3, of which 0 were waited for; matrix products, arithmetic and copies ran while one was open for 0% of the time, Pallas kernels for 0%

profile of v1, /device:TPU:1, one launch (start us, length us, event | category | flops | bytes accessed | tf_op | source)
XLA Modules:
  0.0 112.6 jit_solution(16172727434794332602)
XLA Ops:
  0.0 3.5 %shard_map.82 = (bf16[1040,128]{1,0:T(8,128)(2,1)S(1)}, bf16[128,128]{1,0:T(8,128)(2,1)S(1)}, f32[128,128]{1,0:T(8,128)S(1)}) custom-call(bf16[128,32,384]{2,1,0:T(8,128)(2,1)} %bitcast.28, f32[12,1,128]{2,1,0:T(1,128)} %bitcast.31, s32[32,128]{1,0:T(8,128)} %bitcast.30, s32[1,64]{1,0:T(1,128)} %bitcast.32, s32[1,128]{1,0:T(1,128)} %bitcast.33, ...), custom_call_target="tpu_custom_call" | custom-call | flops 1000000 | bytes 1048576 | tf_op jit(solution)/shard_map/pallas_call | solution.py:244
  3.5 1.3 %collective-permute-start.2 = (bf16[1040,128]{1,0:T(8,128)(2,1)S(1)}, bf16[1040,128]{1,0:T(8,128)(2,1)S(1)}, u32[]{:S(2)}, u32[]{:S(2)}) collective-permute-start(bf16[1040,128]{1,0:T(8,128)(2,1)S(1)} %get-tuple-element.12.w0), channel_id=1, source_target_pairs={{128,256},{192,320},{256,128},{320,192},{384,0},{448,64},{129,257}... | collective-permute-start | bytes 798728 | tf_op jit(solution)/shard_map/ppermute | solution.py:269
  4.8 6.3 %collective-permute-start.1 = (bf16[1040,128]{1,0:T(8,128)(2,1)S(1)}, bf16[1040,128]{1,0:T(8,128)(2,1)S(1)}, u32[]{:S(2)}, u32[]{:S(2)}) collective-permute-start(bf16[1040,128]{1,0:T(8,128)(2,1)S(1)} %get-tuple-element.12.w0), channel_id=1, source_target_pairs={{0,256},{64,320},{256,0},{320,64},{384,128},{448,192},{1,257},{65,... | collective-permute-start | bytes 798728 | tf_op jit(solution)/shard_map/ppermute | solution.py:269
  11.1 1.9 %collective-permute-start = (bf16[1040,128]{1,0:T(8,128)(2,1)S(1)}, bf16[1040,128]{1,0:T(8,128)(2,1)S(1)}, u32[]{:S(2)}, u32[]{:S(2)}) collective-permute-start(bf16[1040,128]{1,0:T(8,128)(2,1)S(1)} %get-tuple-element.12.w0), channel_id=1, source_target_pairs={{0,128},{64,192},{128,0},{192,64},{384,256},{448,320},{1,129},{65,... | collective-permute-start | bytes 798728 | tf_op jit(solution)/shard_map/ppermute | solution.py:269
  13.1 27.0 %all_to_all.30 = bf16[64,2,128]{2,1,0:T(2,128)(2,1)S(1)} all-to-all(bf16[64,2,128]{2,1,0:T(2,128)(2,1)S(1)} %bitcast.27), channel_id=1, replica_groups=mesh['x'=4,'core'=2,'ka'=64] {'ka'}, dimensions={0} | all-to-all | bytes 65536 | tf_op jit(solution)/shard_map/all_to_all | solution.py:234
  40.1 0.2 shard_map.83
  40.3 10.7 %all_to_all.31.parts_ref = bf16[8,40,128]{2,1,0:T(8,128)(2,1)S(1)} all-to-all(bf16[8,40,128]{2,1,0:T(8,128)(2,1)S(1)} %shard_map.83), channel_id=1, replica_groups=mesh['x'=4,'core'=2,'ka'=64] {'x','core'}, dimensions={0} | all-to-all | bytes 163840 | tf_op jit(solution)/shard_map/all_to_all | solution.py:271
  51.0 0.0 collective-permute-done.2.w3
  51.0 0.0 collective-permute-done.1.w2
  51.0 0.0 collective-permute-done.w1
  51.0 0.5 shard_map.84
  51.4 17.6 %all_to_all.32 = bf16[128,2,128]{2,1,0:T(2,128)(2,1)S(1)} all-to-all(bf16[128,2,128]{2,1,0:T(2,128)(2,1)S(1)} %bitcast.26), channel_id=1, replica_groups=mesh['x'=4,'core'=2,'ka'=64] {'core','ka'}, dimensions={0} | all-to-all | bytes 131072 | tf_op jit(solution)/shard_map/all_to_all | solution.py:234
  69.1 0.7 shard_map.85
  69.7 17.6 %all_to_all.33 = bf16[128,2,128]{2,1,0:T(2,128)(2,1)S(1)} all-to-all(bf16[128,2,128]{2,1,0:T(2,128)(2,1)S(1)} %bitcast.22), channel_id=1, replica_groups=mesh['x'=4,'core'=2,'ka'=64] {'core','ka'}, dimensions={0} | all-to-all | bytes 131072 | tf_op jit(solution)/shard_map/all_to_all | solution.py:234
  87.3 0.7 shard_map.86
  88.0 14.7 %all_to_all.34 = bf16[64,2,128]{2,1,0:T(2,128)(2,1)S(1)} all-to-all(bf16[64,2,128]{2,1,0:T(2,128)(2,1)S(1)} %bitcast.23), channel_id=1, replica_groups=mesh['x'=4,'core'=2,'ka'=64] {'ka'}, dimensions={0} | all-to-all | bytes 65536 | tf_op jit(solution)/shard_map/all_to_all | solution.py:234
  102.6 0.2 shard_map.87
  102.9 9.1 %all_to_all.35.parts_ref = bf16[8,32,128]{2,1,0:T(8,128)(2,1)S(1)} all-to-all(bf16[8,32,128]{2,1,0:T(8,128)(2,1)S(1)} %shard_map.87), channel_id=1, replica_groups=mesh['x'=4,'core'=2,'ka'=64] {'x','core'}, dimensions={0} | all-to-all | bytes 131072 | tf_op jit(solution)/shard_map/all_to_all | solution.py:282
  112.0 0.6 shard_map.88
Async XLA Ops:
  3.5 47.5 %collective-permute-start.2 = (bf16[1040,128]{1,0:T(8,128)(2,1)S(1)}, bf16[1040,128]{1,0:T(8,128)(2,1)S(1)}, u32[]{:S(2)}, u32[]{:S(2)}) collective-permute-start(bf16[1040,128]{1,0:T(8,128)(2,1)S(1)} %get-tuple-element.12.w0), channel_id=1, source_target_pairs={{128,256},{192,320},{256,128},{320,192},{384,0},{448,64},{129,257}... | collective-permute-start | bytes 798728 | tf_op jit(solution)/shard_map/ppermute | solution.py:269
  4.8 46.2 %collective-permute-start.1 = (bf16[1040,128]{1,0:T(8,128)(2,1)S(1)}, bf16[1040,128]{1,0:T(8,128)(2,1)S(1)}, u32[]{:S(2)}, u32[]{:S(2)}) collective-permute-start(bf16[1040,128]{1,0:T(8,128)(2,1)S(1)} %get-tuple-element.12.w0), channel_id=1, source_target_pairs={{0,256},{64,320},{256,0},{320,64},{384,128},{448,192},{1,257},{65,... | collective-permute-start | bytes 798728 | tf_op jit(solution)/shard_map/ppermute | solution.py:269
  11.1 39.8 %collective-permute-start = (bf16[1040,128]{1,0:T(8,128)(2,1)S(1)}, bf16[1040,128]{1,0:T(8,128)(2,1)S(1)}, u32[]{:S(2)}, u32[]{:S(2)}) collective-permute-start(bf16[1040,128]{1,0:T(8,128)(2,1)S(1)} %get-tuple-element.12.w0), channel_id=1, source_target_pairs={{0,128},{64,192},{128,0},{192,64},{384,256},{448,320},{1,129},{65,... | collective-permute-start | bytes 798728 | tf_op jit(solution)/shard_map/ppermute | solution.py:269

commit v2 on v1

--- a/solution.py
+++ b/solution.py
@@ -176,7 +176,7 @@
         total = total + parts_ref[p, pl.ds(0, BANDS), :].astype(F32)
     for g in range(4):
         for core in range(2):
-            peer = 2 * jnp.bitwise_xor(lax.axis_index("x"), g) + core
+            peer = 2 * lax.rem(lax.axis_index("x") + 4 - g, 4) + core
             row = parts_ref[peer, pl.ds(BANDS, 8), :].astype(F32)[0:1, :]
             target_ref[pl.ds(2 * g + core, 1), :] = row
     deviation = next_direction(state_ref, total)
@@ -265,8 +265,10 @@
     )))
     arrived = over_owners(terms, "ka")
     weights = [wide]
-    for flip in (2, 4, 6):
-        weights.append(lax.ppermute(wide, PB, [(p, p ^ flip) for p in range(groups) if p ^ flip < 6]))
+    left = lax.ppermute(wide, PB, [(p, (p + 2) % groups) for p in range(groups)])
+    right = lax.ppermute(wide, PB, [(p, p - 2) for p in range(2, groups)])
+    far = lax.ppermute(left, PB, [(p, (p + 2) % groups) for p in (0, 1, 2, 3, 6, 7)])
+    weights += [left, far, right]
     (copies,) = call(receive_kernel, [VMEM], [((groups, BANDS + 8, TILES), BF16)])(arrived)
     parts = lax.all_to_all(copies, PB, split_axis=0, concat_axis=0, tiled=True)
     terms, targets = call(

time: 113 us -> 118 us (1.044)
  waiting for transfers between devices: 0.01 us -> 3.76 us
  blocking collectives: 96.6 us -> 99.1 us
  starting transfers between devices: 9.55 us -> 8.33 us
    ppermute x3, waiting for transfers between devices: 0.01 us -> 3.76 us  [the longest x1 3.76 us: shards(): lax.ppermute(wide, PB, [(p, (p + 2) % groups) for p in range(groups)])]
    all_to_all x2, blocking collectives: 19.8 us -> 21.3 us  [shards(): parts = lax.all_to_all(copies, PB, split_axis=0, concat_axis=0, tiled=True)]
    ppermute x3, starting transfers between devices: 9.55 us -> 8.33 us  [the longest x1 3.94 us: shards(): lax.ppermute(wide, PB, [(p, (p + 2) % groups) for p in range(groups)])]
  transfers between devices with their start and end apart: 3 -> 3, of which waited for: 0 -> 1; matrix products, arithmetic and copies ran while one was open for 0% -> 0% of each run, Pallas kernels for 0% -> 0%
where the time goes in v2:
time: 118 us
  blocking collectives  99.1 us (84%)
  starting transfers between devices  8.33 us (7%)
  Pallas kernels  6.34 us (5%)
  waiting for transfers between devices  3.76 us (3%)
    all_to_all x4, blocking collectives, over_owners(): lax.all_to_all(terms.reshape(-1, TILE_SLOTS, TILES), axes, split_axis=0,...  77.9 us
    all_to_all x2, blocking collectives, shards(): parts = lax.all_to_all(copies, PB, split_axis=0, concat_axis=0, tiled=True)  21.3 us
    ppermute x1, starting transfers between devices, shards(): lax.ppermute(wide, PB, [(p, (p + 2) % groups) for p in range(groups)])  3.94 us
    ppermute x1, waiting for transfers between devices, shards(): lax.ppermute(wide, PB, [(p, (p + 2) % groups) for p in range(groups)])  3.76 us
    pallas_call x1, Pallas kernels, shards(): call(weight_kernel, [pl.BlockSpec(memory_space=pltpu.HBM)] * 8, [((WIDE +...  3.48 us
    ppermute x1, starting transfers between devices, shards(): lax.ppermute(left, PB, [(p, (p + 2) % groups) for p in (0, 1, 2, 3, 6, 7)])  3.1 us
  transfers between devices with their start and end apart: 3, of which 1 were waited for; matrix products, arithmetic and copies ran while one was open for 0% of the time, Pallas kernels for 0%

profile of v2, /device:TPU:1, one launch (start us, length us, event | category | flops | bytes accessed | tf_op | source)
XLA Modules:
  0.0 117.7 jit_solution(842003153368085572)
XLA Ops:
  0.0 3.5 %shard_map.82 = (bf16[1040,128]{1,0:T(8,128)(2,1)S(1)}, bf16[128,128]{1,0:T(8,128)(2,1)S(1)}, f32[128,128]{1,0:T(8,128)S(1)}) custom-call(bf16[128,32,384]{2,1,0:T(8,128)(2,1)} %bitcast.28, f32[12,1,128]{2,1,0:T(1,128)} %bitcast.31, s32[32,128]{1,0:T(8,128)} %bitcast.30, s32[1,64]{1,0:T(1,128)} %bitcast.32, s32[1,128]{1,0:T(1,128)} %bitcast.33, ...), custom_call_target="tpu_custom_call" | custom-call | flops 1000000 | bytes 1048576 | tf_op jit(solution)/shard_map/pallas_call | solution.py:244
  3.5 3.9 %collective-permute-start = (bf16[1040,128]{1,0:T(8,128)(2,1)S(1)}, bf16[1040,128]{1,0:T(8,128)(2,1)S(1)}, u32[]{:S(2)}, u32[]{:S(2)}) collective-permute-start(bf16[1040,128]{1,0:T(8,128)(2,1)S(1)} %get-tuple-element.12.w0), channel_id=1, source_target_pairs={{0,128},{64,192},{128,256},{192,320},{256,384},{320,448},{384,0},{... | collective-permute-start | bytes 798728 | tf_op jit(solution)/shard_map/ppermute | solution.py:268
  7.4 1.3 %collective-permute-start.2 = (bf16[1040,128]{1,0:T(8,128)(2,1)S(1)}, bf16[1040,128]{1,0:T(8,128)(2,1)S(1)}, u32[]{:S(2)}, u32[]{:S(2)}) collective-permute-start(bf16[1040,128]{1,0:T(8,128)(2,1)S(1)} %get-tuple-element.12.w0), channel_id=1, source_target_pairs={{128,0},{192,64},{256,128},{320,192},{384,256},{448,320},{129,1},{... | collective-permute-start | bytes 798728 | tf_op jit(solution)/shard_map/ppermute | solution.py:269
  8.7 3.8 %collective-permute-done.w1 = bf16[1040,128]{1,0:T(8,128)(2,1)S(1)} collective-permute-done((bf16[1040,128]{1,0:T(8,128)(2,1)S(1)}, bf16[1040,128]{1,0:T(8,128)(2,1)S(1)}, u32[]{:S(2)}, u32[]{:S(2)}) %collective-permute-start) | collective-permute-done | bytes 266272 | tf_op jit(solution)/shard_map/ppermute | solution.py:268
  12.5 3.1 %collective-permute-start.1 = (bf16[1040,128]{1,0:T(8,128)(2,1)S(1)}, bf16[1040,128]{1,0:T(8,128)(2,1)S(1)}, u32[]{:S(2)}, u32[]{:S(2)}) collective-permute-start(bf16[1040,128]{1,0:T(8,128)(2,1)S(1)} %collective-permute-done.w1), channel_id=1, source_target_pairs={{0,128},{64,192},{128,256},{192,320},{384,0},{448,64},{1,129},{65,... | collective-permute-start | bytes 798728 | tf_op jit(solution)/shard_map/ppermute | solution.py:270
  15.6 28.0 %all_to_all.30 = bf16[64,2,128]{2,1,0:T(2,128)(2,1)S(1)} all-to-all(bf16[64,2,128]{2,1,0:T(2,128)(2,1)S(1)} %bitcast.27), channel_id=1, replica_groups=mesh['x'=4,'core'=2,'ka'=64] {'ka'}, dimensions={0} | all-to-all | bytes 65536 | tf_op jit(solution)/shard_map/all_to_all | solution.py:234
  43.6 0.2 shard_map.83
  43.8 12.2 %all_to_all.31.parts_ref = bf16[8,40,128]{2,1,0:T(8,128)(2,1)S(1)} all-to-all(bf16[8,40,128]{2,1,0:T(8,128)(2,1)S(1)} %shard_map.83), channel_id=1, replica_groups=mesh['x'=4,'core'=2,'ka'=64] {'x','core'}, dimensions={0} | all-to-all | bytes 163840 | tf_op jit(solution)/shard_map/all_to_all | solution.py:273
  56.0 0.0 collective-permute-done.2.w3
  56.0 0.0 collective-permute-done.1.w2
  56.0 0.5 shard_map.84
  56.5 17.6 %all_to_all.32 = bf16[128,2,128]{2,1,0:T(2,128)(2,1)S(1)} all-to-all(bf16[128,2,128]{2,1,0:T(2,128)(2,1)S(1)} %bitcast.26), channel_id=1, replica_groups=mesh['x'=4,'core'=2,'ka'=64] {'core','ka'}, dimensions={0} | all-to-all | bytes 131072 | tf_op jit(solution)/shard_map/all_to_all | solution.py:234
  74.1 0.7 shard_map.85
  74.8 17.6 %all_to_all.33 = bf16[128,2,128]{2,1,0:T(2,128)(2,1)S(1)} all-to-all(bf16[128,2,128]{2,1,0:T(2,128)(2,1)S(1)} %bitcast.22), channel_id=1, replica_groups=mesh['x'=4,'core'=2,'ka'=64] {'core','ka'}, dimensions={0} | all-to-all | bytes 131072 | tf_op jit(solution)/shard_map/all_to_all | solution.py:234
  92.4 0.7 shard_map.86
  93.0 14.7 %all_to_all.34 = bf16[64,2,128]{2,1,0:T(2,128)(2,1)S(1)} all-to-all(bf16[64,2,128]{2,1,0:T(2,128)(2,1)S(1)} %bitcast.23), channel_id=1, replica_groups=mesh['x'=4,'core'=2,'ka'=64] {'ka'}, dimensions={0} | all-to-all | bytes 65536 | tf_op jit(solution)/shard_map/all_to_all | solution.py:234
  107.7 0.2 shard_map.87
  107.9 9.1 %all_to_all.35.parts_ref = bf16[8,32,128]{2,1,0:T(8,128)(2,1)S(1)} all-to-all(bf16[8,32,128]{2,1,0:T(8,128)(2,1)S(1)} %shard_map.87), channel_id=1, replica_groups=mesh['x'=4,'core'=2,'ka'=64] {'x','core'}, dimensions={0} | all-to-all | bytes 131072 | tf_op jit(solution)/shard_map/all_to_all | solution.py:284
  117.0 0.6 shard_map.88
Async XLA Ops:
  3.5 9.0 %collective-permute-start = (bf16[1040,128]{1,0:T(8,128)(2,1)S(1)}, bf16[1040,128]{1,0:T(8,128)(2,1)S(1)}, u32[]{:S(2)}, u32[]{:S(2)}) collective-permute-start(bf16[1040,128]{1,0:T(8,128)(2,1)S(1)} %get-tuple-element.12.w0), channel_id=1, source_target_pairs={{0,128},{64,192},{128,256},{192,320},{256,384},{320,448},{384,0},{... | collective-permute-start | bytes 798728 | tf_op jit(solution)/shard_map/ppermute | solution.py:268
  7.4 48.6 %collective-permute-start.2 = (bf16[1040,128]{1,0:T(8,128)(2,1)S(1)}, bf16[1040,128]{1,0:T(8,128)(2,1)S(1)}, u32[]{:S(2)}, u32[]{:S(2)}) collective-permute-start(bf16[1040,128]{1,0:T(8,128)(2,1)S(1)} %get-tuple-element.12.w0), channel_id=1, source_target_pairs={{128,0},{192,64},{256,128},{320,192},{384,256},{448,320},{129,1},{... | collective-permute-start | bytes 798728 | tf_op jit(solution)/shard_map/ppermute | solution.py:269
  12.5 43.5 %collective-permute-start.1 = (bf16[1040,128]{1,0:T(8,128)(2,1)S(1)}, bf16[1040,128]{1,0:T(8,128)(2,1)S(1)}, u32[]{:S(2)}, u32[]{:S(2)}) collective-permute-start(bf16[1040,128]{1,0:T(8,128)(2,1)S(1)} %collective-permute-done.w1), channel_id=1, source_target_pairs={{0,128},{64,192},{128,256},{192,320},{384,0},{448,64},{1,129},{65,... | collective-permute-start | bytes 798728 | tf_op jit(solution)/shard_map/ppermute | solution.py:270

commit v3 on v2

--- a/solution.py
+++ b/solution.py
@@ -54,11 +54,11 @@
 def weight_kernel(
     coupling, occ, window, count, source, target, velocity, lifetime,
     wide_ref, out_ref, state_ref,
-    weight_ref, index_ref, tiles, flat, occ_wide, occ_pad, window_ref, count_ref, mask_ref, chosen_ref, half_ref, term_ref, sems, small_sems,
+    weight_ref, index_ref, tiles, flat, occ_wide, occ_rows_ref, occ_pad, window_ref, count_ref, mask_ref, chosen_ref, half_ref, term_ref, sems, small_sems,
 ):
     small = []
     for place, (origin, into) in enumerate((
-        *((occ.at[v], occ_pad.at[pl.ds(v, 1)]) for v in range(MODES)),
+        (occ, occ_rows_ref),
         (count, count_ref),
         (window, window_ref),
         (velocity, state_ref.at[pl.ds(0, ROWS)]),
@@ -74,15 +74,17 @@
         copies.append(pltpu.make_async_copy(coupling.at[part], tiles.at[part], sems.at[c]))
         copies[-1].start()
         if c == 0:
-            for copy in small[:MODES]:
+            for copy in small[:1]:
                 copy.start()
-    for copy in small[MODES:]:
+    for copy in small[1:]:
         copy.start()
     spread = (iota((16, LANES), 1) % MODES == iota((16, LANES), 0)).astype(F32).astype(BF16)
     gather = (iota((LANES, TILES), 0) // MODES == iota((LANES, TILES), 1) // 4).astype(F32).astype(BF16)
     group = iota((1, TILES), 1) % 4
-    for copy in small[:MODES]:
+    for copy in small[:1]:
         copy.wait()
+    for v in range(MODES):
+        occ_pad[pl.ds(v, 1), :] = occ_rows_ref[v]
     valid = iota((16, TILES), 0) < MODES
     occ_rows = jnp.where(valid, occ_pad[...], 0.0).T.astype(BF16)
     occ_wide[...] = jnp.dot(occ_rows, spread, preferred_element_type=F32)
@@ -100,7 +102,7 @@
                 row = t * BANDS + j * 8
                 merged = jnp.where(group == j, summed[row : row + 8, :], merged)
             flat[pl.ds((begin[c] + t) * 8, 8), :] = merged
-    for copy in small[MODES:]:
+    for copy in small[1:]:
         copy.wait()
     count = count_ref[...].astype(F32).astype(BF16)
     owner = (iota((64, TILES), 1) // TILE_SLOTS == iota((64, TILES), 0)).astype(F32).astype(BF16)
@@ -250,13 +252,14 @@
             pltpu.VMEM((TILES, BANDS, LANES), BF16),
             pltpu.VMEM((TILES * 8, TILES), F32),
             pltpu.VMEM((TILES, LANES), F32),
+            pltpu.VMEM((MODES, 1, TILES), F32),
             pltpu.VMEM((16, TILES), F32),
             pltpu.VMEM((BANDS, TILES), jnp.int32),
             pltpu.VMEM((1, 64), jnp.int32),
             pltpu.VMEM((2 * BANDS, TILES), F32),
             pltpu.VMEM((ROWS, TILES), F32), *small[1:],
             pltpu.SemaphoreType.DMA((len(CHUNKS),)),
-            pltpu.SemaphoreType.DMA((MODES + 6,)),
+            pltpu.SemaphoreType.DMA((7,)),
         ],
         limit=16 << 20,
     )(*(pltpu.with_memory_space_constraint(x, pltpu.HBM) for x in (

time: 118 us -> 118 us (level)
  no operation moved by 1% of the time
where the time goes in v3:
time: 118 us; the launch traced here: 117 us
  blocking collectives  99.1 us (84%)
  starting transfers between devices  8.34 us (7%)
  Pallas kernels  6.16 us (5%)
  waiting for transfers between devices  3.76 us (3%)
    all_to_all x4, blocking collectives, over_owners(): lax.all_to_all(terms.reshape(-1, TILE_SLOTS, TILES), axes, split_axis=0,...  77.9 us
    all_to_all x2, blocking collectives, shards(): parts = lax.all_to_all(copies, PB, split_axis=0, concat_axis=0, tiled=True)  21.3 us
    ppermute x1, starting transfers between devices, shards(): lax.ppermute(wide, PB, [(p, (p + 2) % groups) for p in range(groups)])  3.94 us
    ppermute x1, waiting for transfers between devices, shards(): lax.ppermute(wide, PB, [(p, (p + 2) % groups) for p in range(groups)])  3.76 us
    pallas_call x1, Pallas kernels, shards(): call(weight_kernel, [pl.BlockSpec(memory_space=pltpu.HBM)] * 8, [((WIDE +...  3.29 us
    ppermute x1, starting transfers between devices, shards(): lax.ppermute(left, PB, [(p, (p + 2) % groups) for p in (0, 1, 2, 3, 6, 7)])  3.11 us
  transfers between devices with their start and end apart: 3, of which 1 were waited for; matrix products, arithmetic and copies ran while one was open for 0% of the time, Pallas kernels for 0%

profile of v3, /device:TPU:1, one launch (start us, length us, event | category | flops | bytes accessed | tf_op | source)
XLA Modules:
  0.0 117.5 jit_solution(8320877768117443301)
XLA Ops:
  0.0 3.3 %shard_map.82 = (bf16[1040,128]{1,0:T(8,128)(2,1)S(1)}, bf16[128,128]{1,0:T(8,128)(2,1)S(1)}, f32[128,128]{1,0:T(8,128)S(1)}) custom-call(bf16[128,32,384]{2,1,0:T(8,128)(2,1)} %bitcast.28, f32[12,1,128]{2,1,0:T(1,128)} %bitcast.31, s32[32,128]{1,0:T(8,128)} %bitcast.30, s32[1,64]{1,0:T(1,128)} %bitcast.32, s32[1,128]{1,0:T(1,128)} %bitcast.33, ...), custom_call_target="tpu_custom_call" | custom-call | flops 1000000 | bytes 1048576 | tf_op jit(solution)/shard_map/pallas_call | solution.py:246
  3.3 3.9 %collective-permute-start = (bf16[1040,128]{1,0:T(8,128)(2,1)S(1)}, bf16[1040,128]{1,0:T(8,128)(2,1)S(1)}, u32[]{:S(2)}, u32[]{:S(2)}) collective-permute-start(bf16[1040,128]{1,0:T(8,128)(2,1)S(1)} %get-tuple-element.12.w0), channel_id=1, source_target_pairs={{0,128},{64,192},{128,256},{192,320},{256,384},{320,448},{384,0},{... | collective-permute-start | bytes 798728 | tf_op jit(solution)/shard_map/ppermute | solution.py:271
  7.2 1.3 %collective-permute-start.2 = (bf16[1040,128]{1,0:T(8,128)(2,1)S(1)}, bf16[1040,128]{1,0:T(8,128)(2,1)S(1)}, u32[]{:S(2)}, u32[]{:S(2)}) collective-permute-start(bf16[1040,128]{1,0:T(8,128)(2,1)S(1)} %get-tuple-element.12.w0), channel_id=1, source_target_pairs={{128,0},{192,64},{256,128},{320,192},{384,256},{448,320},{129,1},{... | collective-permute-start | bytes 798728 | tf_op jit(solution)/shard_map/ppermute | solution.py:272
  8.5 3.8 %collective-permute-done.w1 = bf16[1040,128]{1,0:T(8,128)(2,1)S(1)} collective-permute-done((bf16[1040,128]{1,0:T(8,128)(2,1)S(1)}, bf16[1040,128]{1,0:T(8,128)(2,1)S(1)}, u32[]{:S(2)}, u32[]{:S(2)}) %collective-permute-start) | collective-permute-done | bytes 266272 | tf_op jit(solution)/shard_map/ppermute | solution.py:271
  12.3 3.1 %collective-permute-start.1 = (bf16[1040,128]{1,0:T(8,128)(2,1)S(1)}, bf16[1040,128]{1,0:T(8,128)(2,1)S(1)}, u32[]{:S(2)}, u32[]{:S(2)}) collective-permute-start(bf16[1040,128]{1,0:T(8,128)(2,1)S(1)} %collective-permute-done.w1), channel_id=1, source_target_pairs={{0,128},{64,192},{128,256},{192,320},{384,0},{448,64},{1,129},{65,... | collective-permute-start | bytes 798728 | tf_op jit(solution)/shard_map/ppermute | solution.py:273
  15.4 28.0 %all_to_all.30 = bf16[64,2,128]{2,1,0:T(2,128)(2,1)S(1)} all-to-all(bf16[64,2,128]{2,1,0:T(2,128)(2,1)S(1)} %bitcast.27), channel_id=1, replica_groups=mesh['x'=4,'core'=2,'ka'=64] {'ka'}, dimensions={0} | all-to-all | bytes 65536 | tf_op jit(solution)/shard_map/all_to_all | solution.py:236
  43.4 0.2 shard_map.83
  43.6 12.2 %all_to_all.31.parts_ref = bf16[8,40,128]{2,1,0:T(8,128)(2,1)S(1)} all-to-all(bf16[8,40,128]{2,1,0:T(8,128)(2,1)S(1)} %shard_map.83), channel_id=1, replica_groups=mesh['x'=4,'core'=2,'ka'=64] {'x','core'}, dimensions={0} | all-to-all | bytes 163840 | tf_op jit(solution)/shard_map/all_to_all | solution.py:276
  55.8 0.0 collective-permute-done.2.w3
  55.8 0.0 collective-permute-done.1.w2
  55.8 0.5 shard_map.84
  56.3 17.6 %all_to_all.32 = bf16[128,2,128]{2,1,0:T(2,128)(2,1)S(1)} all-to-all(bf16[128,2,128]{2,1,0:T(2,128)(2,1)S(1)} %bitcast.26), channel_id=1, replica_groups=mesh['x'=4,'core'=2,'ka'=64] {'core','ka'}, dimensions={0} | all-to-all | bytes 131072 | tf_op jit(solution)/shard_map/all_to_all | solution.py:236
  73.9 0.7 shard_map.85
  74.6 17.6 %all_to_all.33 = bf16[128,2,128]{2,1,0:T(2,128)(2,1)S(1)} all-to-all(bf16[128,2,128]{2,1,0:T(2,128)(2,1)S(1)} %bitcast.22), channel_id=1, replica_groups=mesh['x'=4,'core'=2,'ka'=64] {'core','ka'}, dimensions={0} | all-to-all | bytes 131072 | tf_op jit(solution)/shard_map/all_to_all | solution.py:236
  92.2 0.7 shard_map.86
  92.9 14.7 %all_to_all.34 = bf16[64,2,128]{2,1,0:T(2,128)(2,1)S(1)} all-to-all(bf16[64,2,128]{2,1,0:T(2,128)(2,1)S(1)} %bitcast.23), channel_id=1, replica_groups=mesh['x'=4,'core'=2,'ka'=64] {'ka'}, dimensions={0} | all-to-all | bytes 65536 | tf_op jit(solution)/shard_map/all_to_all | solution.py:236
  107.5 0.2 shard_map.87
  107.7 9.1 %all_to_all.35.parts_ref = bf16[8,32,128]{2,1,0:T(8,128)(2,1)S(1)} all-to-all(bf16[8,32,128]{2,1,0:T(8,128)(2,1)S(1)} %shard_map.87), channel_id=1, replica_groups=mesh['x'=4,'core'=2,'ka'=64] {'x','core'}, dimensions={0} | all-to-all | bytes 131072 | tf_op jit(solution)/shard_map/all_to_all | solution.py:287
  116.8 0.6 shard_map.88
Async XLA Ops:
  3.3 9.0 %collective-permute-start = (bf16[1040,128]{1,0:T(8,128)(2,1)S(1)}, bf16[1040,128]{1,0:T(8,128)(2,1)S(1)}, u32[]{:S(2)}, u32[]{:S(2)}) collective-permute-start(bf16[1040,128]{1,0:T(8,128)(2,1)S(1)} %get-tuple-element.12.w0), channel_id=1, source_target_pairs={{0,128},{64,192},{128,256},{192,320},{256,384},{320,448},{384,0},{... | collective-permute-start | bytes 798728 | tf_op jit(solution)/shard_map/ppermute | solution.py:271
  7.2 48.6 %collective-permute-start.2 = (bf16[1040,128]{1,0:T(8,128)(2,1)S(1)}, bf16[1040,128]{1,0:T(8,128)(2,1)S(1)}, u32[]{:S(2)}, u32[]{:S(2)}) collective-permute-start(bf16[1040,128]{1,0:T(8,128)(2,1)S(1)} %get-tuple-element.12.w0), channel_id=1, source_target_pairs={{128,0},{192,64},{256,128},{320,192},{384,256},{448,320},{129,1},{... | collective-permute-start | bytes 798728 | tf_op jit(solution)/shard_map/ppermute | solution.py:272
  12.3 43.5 %collective-permute-start.1 = (bf16[1040,128]{1,0:T(8,128)(2,1)S(1)}, bf16[1040,128]{1,0:T(8,128)(2,1)S(1)}, u32[]{:S(2)}, u32[]{:S(2)}) collective-permute-start(bf16[1040,128]{1,0:T(8,128)(2,1)S(1)} %collective-permute-done.w1), channel_id=1, source_target_pairs={{0,128},{64,192},{128,256},{192,320},{384,0},{448,64},{1,129},{65,... | collective-permute-start | bytes 798728 | tf_op jit(solution)/shard_map/ppermute | solution.py:273

commit v4 on v3

--- a/solution.py
+++ b/solution.py
@@ -148,12 +148,8 @@
         out_ref[p] = messages[p // 2 % 3]
 
 
-def direction_terms(deviation, weights, chosen_ref, half_ref, term_ref, out_ref):
-    picks = []
-    for weight in weights:
-        source_row = weight[pl.ds(WIDE, 16), :].astype(F32)[0:1, :].astype(jnp.int32)
-        picks.append(onehot(iota((TILES, TILES), 0) == source_row))
-    chosen = jnp.dot(deviation.astype(BF16), jnp.concatenate(picks, axis=1), preferred_element_type=F32)
+def direction_terms(deviation, picks, weights, chosen_ref, half_ref, term_ref, out_ref):
+    chosen = jnp.dot(deviation.astype(BF16), picks, preferred_element_type=F32)
     for g, weight in enumerate(weights):
         chosen_ref[pl.ds(g * BANDS, BANDS), :] = chosen[:, g * TILES : (g + 1) * TILES]
     for g, weight in enumerate(weights):
@@ -172,40 +168,44 @@
     return state_ref[pl.ds(ROWS, BANDS), :] * (state_ref[rows, :] + scattering)
 
 
-def first_kernel(parts_ref, state_ref, w0, w1, w2, w3, out_ref, target_ref, chosen_ref, half_ref, term_ref):
+def first_kernel(parts_ref, state_ref, w0, w1, w2, w3, out_ref, place_ref, pick_ref, chosen_ref, half_ref, term_ref):
     total = parts_ref[0, pl.ds(0, BANDS), :].astype(F32)
     for p in range(1, parts_ref.shape[0]):
         total = total + parts_ref[p, pl.ds(0, BANDS), :].astype(F32)
     for g in range(4):
         for core in range(2):
             peer = 2 * lax.rem(lax.axis_index("x") + 4 - g, 4) + core
-            row = parts_ref[peer, pl.ds(BANDS, 8), :].astype(F32)[0:1, :]
-            target_ref[pl.ds(2 * g + core, 1), :] = row
+            target = parts_ref[peer, pl.ds(BANDS, 8), :].astype(F32)[0:1, :].astype(jnp.int32)
+            columns = pl.ds((2 * g + core) * TILES, TILES)
+            place_ref[:, columns] = onehot(iota((TILES, TILES), 0) == target)
+    for g, weight in enumerate((w0, w1, w2, w3)):
+        source_row = weight[pl.ds(WIDE, 16), :].astype(F32)[0:1, :].astype(jnp.int32)
+        pick_ref[:, pl.ds(g * TILES, TILES)] = onehot(iota((TILES, TILES), 0) == source_row)
     deviation = next_direction(state_ref, total)
-    direction_terms(deviation, (w0, w1, w2, w3), chosen_ref, half_ref, term_ref, out_ref)
-
-
-def direction_sum(terms_ref, target_ref, cores):
+    direction_terms(deviation, pick_ref[...], (w0, w1, w2, w3), chosen_ref, half_ref, term_ref, out_ref)
+
+
+def direction_sum(terms_ref, place_ref, cores):
     turned = terms_ref[...].astype(F32).T.astype(BF16)
     left, right = [], []
     for g in range(4):
         left.append(turned[g * BANDS : (g + 1) * BANDS, :])
         for core in cores:
-            target = target_ref[pl.ds(2 * g + core, 1), :].astype(jnp.int32)
-            right.append(onehot(iota((TILES, TILES), 0) == target))
+            start = (2 * g + core) * TILES
+            right.append(place_ref[:, pl.ds(pl.multiple_of(start, TILES), TILES)])
     return lax.dot_general(
         jnp.concatenate(left, axis=1), jnp.concatenate(right, axis=1), (((1,), (1,)), ((), ())),
         preferred_element_type=F32,
     )
 
 
-def step_kernel(terms_ref, target_ref, state_ref, w0, w1, w2, w3, out_ref, chosen_ref, half_ref, term_ref):
-    deviation = next_direction(state_ref, direction_sum(terms_ref, target_ref, (0, 1)))
-    direction_terms(deviation, (w0, w1, w2, w3), chosen_ref, half_ref, term_ref, out_ref)
-
-
-def last_kernel(terms_ref, target_ref, out_ref):
-    total = direction_sum(terms_ref, target_ref, (lax.axis_index("core"),)).astype(BF16)
+def step_kernel(terms_ref, place_ref, pick_ref, state_ref, w0, w1, w2, w3, out_ref, chosen_ref, half_ref, term_ref):
+    deviation = next_direction(state_ref, direction_sum(terms_ref, place_ref, (0, 1)))
+    direction_terms(deviation, pick_ref[...], (w0, w1, w2, w3), chosen_ref, half_ref, term_ref, out_ref)
+
+
+def last_kernel(terms_ref, place_ref, out_ref):
+    total = direction_sum(terms_ref, place_ref, (lax.axis_index("core"),)).astype(BF16)
     for p in range(out_ref.shape[0]):
         out_ref[p] = total
 
@@ -274,16 +274,16 @@
     weights += [left, far, right]
     (copies,) = call(receive_kernel, [VMEM], [((groups, BANDS + 8, TILES), BF16)])(arrived)
     parts = lax.all_to_all(copies, PB, split_axis=0, concat_axis=0, tiled=True)
-    terms, targets = call(
-        first_kernel, [VMEM] * 6, [((2, TILES, TILES), BF16), ((8, TILES), F32)], small
+    terms, places, picks = call(
+        first_kernel, [VMEM] * 6, [((2, TILES, TILES), BF16), ((TILES, 8 * TILES), BF16), ((TILES, 4 * TILES), BF16)], small
     )(parts, state, *weights)
     for copied in (2, 1):
         arrived = over_owners(terms, ("core", "ka"))
-        (terms,) = call(step_kernel, [VMEM] * 7, [((copied, TILES, TILES), BF16)], small)(
-            arrived, targets, state, *weights
+        (terms,) = call(step_kernel, [VMEM] * 8, [((copied, TILES, TILES), BF16)], small)(
+            arrived, places, picks, state, *weights
         )
     arrived = over_owners(terms, "ka")
-    (copies,) = call(last_kernel, [VMEM] * 2, [((groups, BANDS, TILES), BF16)])(arrived, targets)
+    (copies,) = call(last_kernel, [VMEM] * 2, [((groups, BANDS, TILES), BF16)])(arrived, places)
     parts = lax.all_to_all(copies, PB, split_axis=0, concat_axis=0, tiled=True)
     (deviation,) = call(final_kernel, [VMEM] * 2, [((ROWS, TILES), F32)])(parts, state)
     return deviation.reshape(3, BANDS, TILES)

time: 118 us -> 118 us (level)
  no operation moved by 1% of the time
where the time goes in v4:
time: 118 us
  blocking collectives  99.1 us (84%)
  starting transfers between devices  8.34 us (7%)
  Pallas kernels  6.21 us (5%)
  waiting for transfers between devices  3.76 us (3%)
    all_to_all x4, blocking collectives, over_owners(): lax.all_to_all(terms.reshape(-1, TILE_SLOTS, TILES), axes, split_axis=0,...  77.9 us
    all_to_all x2, blocking collectives, shards(): parts = lax.all_to_all(copies, PB, split_axis=0, concat_axis=0, tiled=True)  21.3 us
    ppermute x1, starting transfers between devices, shards(): lax.ppermute(wide, PB, [(p, (p + 2) % groups) for p in range(groups)])  3.94 us
    ppermute x1, waiting for transfers between devices, shards(): lax.ppermute(wide, PB, [(p, (p + 2) % groups) for p in range(groups)])  3.76 us
    pallas_call x1, Pallas kernels, shards(): call(weight_kernel, [pl.BlockSpec(memory_space=pltpu.HBM)] * 8, [((WIDE +...  3.29 us
    ppermute x1, starting transfers between devices, shards(): lax.ppermute(left, PB, [(p, (p + 2) % groups) for p in (0, 1, 2, 3, 6, 7)])  3.11 us
  transfers between devices with their start and end apart: 3, of which 1 were waited for; matrix products, arithmetic and copies ran while one was open for 0% of the time, Pallas kernels for 0%

profile of v4, /device:TPU:1, one launch (start us, length us, event | category | flops | bytes accessed | tf_op | source)
XLA Modules:
  0.0 117.5 jit_solution(8854557240264219637)
XLA Ops:
  0.0 3.3 %shard_map.82 = (bf16[1040,128]{1,0:T(8,128)(2,1)S(1)}, bf16[128,128]{1,0:T(8,128)(2,1)S(1)}, f32[128,128]{1,0:T(8,128)S(1)}) custom-call(bf16[128,32,384]{2,1,0:T(8,128)(2,1)} %bitcast.28, f32[12,1,128]{2,1,0:T(1,128)} %bitcast.31, s32[32,128]{1,0:T(8,128)} %bitcast.30, s32[1,64]{1,0:T(1,128)} %bitcast.32, s32[1,128]{1,0:T(1,128)} %bitcast.33, ...), custom_call_target="tpu_custom_call" | custom-call | flops 1000000 | bytes 1048576 | tf_op jit(solution)/shard_map/pallas_call | solution.py:246
  3.3 3.9 %collective-permute-start = (bf16[1040,128]{1,0:T(8,128)(2,1)S(1)}, bf16[1040,128]{1,0:T(8,128)(2,1)S(1)}, u32[]{:S(2)}, u32[]{:S(2)}) collective-permute-start(bf16[1040,128]{1,0:T(8,128)(2,1)S(1)} %get-tuple-element.13.w0), channel_id=1, source_target_pairs={{0,128},{64,192},{128,256},{192,320},{256,384},{320,448},{384,0},{... | collective-permute-start | bytes 798728 | tf_op jit(solution)/shard_map/ppermute | solution.py:271
  7.2 1.3 %collective-permute-start.2 = (bf16[1040,128]{1,0:T(8,128)(2,1)S(1)}, bf16[1040,128]{1,0:T(8,128)(2,1)S(1)}, u32[]{:S(2)}, u32[]{:S(2)}) collective-permute-start(bf16[1040,128]{1,0:T(8,128)(2,1)S(1)} %get-tuple-element.13.w0), channel_id=1, source_target_pairs={{128,0},{192,64},{256,128},{320,192},{384,256},{448,320},{129,1},{... | collective-permute-start | bytes 798728 | tf_op jit(solution)/shard_map/ppermute | solution.py:272
  8.5 3.8 %collective-permute-done.w1 = bf16[1040,128]{1,0:T(8,128)(2,1)S(1)} collective-permute-done((bf16[1040,128]{1,0:T(8,128)(2,1)S(1)}, bf16[1040,128]{1,0:T(8,128)(2,1)S(1)}, u32[]{:S(2)}, u32[]{:S(2)}) %collective-permute-start) | collective-permute-done | bytes 266272 | tf_op jit(solution)/shard_map/ppermute | solution.py:271
  12.3 3.1 %collective-permute-start.1 = (bf16[1040,128]{1,0:T(8,128)(2,1)S(1)}, bf16[1040,128]{1,0:T(8,128)(2,1)S(1)}, u32[]{:S(2)}, u32[]{:S(2)}) collective-permute-start(bf16[1040,128]{1,0:T(8,128)(2,1)S(1)} %collective-permute-done.w1), channel_id=1, source_target_pairs={{0,128},{64,192},{128,256},{192,320},{384,0},{448,64},{1,129},{65,... | collective-permute-start | bytes 798728 | tf_op jit(solution)/shard_map/ppermute | solution.py:273
  15.4 28.0 %all_to_all.30 = bf16[64,2,128]{2,1,0:T(2,128)(2,1)S(1)} all-to-all(bf16[64,2,128]{2,1,0:T(2,128)(2,1)S(1)} %bitcast.27), channel_id=1, replica_groups=mesh['x'=4,'core'=2,'ka'=64] {'ka'}, dimensions={0} | all-to-all | bytes 65536 | tf_op jit(solution)/shard_map/all_to_all | solution.py:236
  43.4 0.2 shard_map.83
  43.6 12.2 %all_to_all.31.parts_ref = bf16[8,40,128]{2,1,0:T(8,128)(2,1)S(1)} all-to-all(bf16[8,40,128]{2,1,0:T(8,128)(2,1)S(1)} %shard_map.83), channel_id=1, replica_groups=mesh['x'=4,'core'=2,'ka'=64] {'x','core'}, dimensions={0} | all-to-all | bytes 163840 | tf_op jit(solution)/shard_map/all_to_all | solution.py:276
  55.8 0.0 collective-permute-done.2.w3
  55.8 0.0 collective-permute-done.1.w2
  55.8 0.5 shard_map.84
  56.4 17.6 %all_to_all.32 = bf16[128,2,128]{2,1,0:T(2,128)(2,1)S(1)} all-to-all(bf16[128,2,128]{2,1,0:T(2,128)(2,1)S(1)} %bitcast.26), channel_id=1, replica_groups=mesh['x'=4,'core'=2,'ka'=64] {'core','ka'}, dimensions={0} | all-to-all | bytes 131072 | tf_op jit(solution)/shard_map/all_to_all | solution.py:236
  74.0 0.7 shard_map.85
  74.7 17.6 %all_to_all.33 = bf16[128,2,128]{2,1,0:T(2,128)(2,1)S(1)} all-to-all(bf16[128,2,128]{2,1,0:T(2,128)(2,1)S(1)} %bitcast.22), channel_id=1, replica_groups=mesh['x'=4,'core'=2,'ka'=64] {'core','ka'}, dimensions={0} | all-to-all | bytes 131072 | tf_op jit(solution)/shard_map/all_to_all | solution.py:236
  92.2 0.7 shard_map.86
  92.9 14.7 %all_to_all.34 = bf16[64,2,128]{2,1,0:T(2,128)(2,1)S(1)} all-to-all(bf16[64,2,128]{2,1,0:T(2,128)(2,1)S(1)} %bitcast.23), channel_id=1, replica_groups=mesh['x'=4,'core'=2,'ka'=64] {'ka'}, dimensions={0} | all-to-all | bytes 65536 | tf_op jit(solution)/shard_map/all_to_all | solution.py:236
  107.6 0.2 shard_map.87
  107.8 9.1 %all_to_all.35.parts_ref = bf16[8,32,128]{2,1,0:T(8,128)(2,1)S(1)} all-to-all(bf16[8,32,128]{2,1,0:T(8,128)(2,1)S(1)} %shard_map.87), channel_id=1, replica_groups=mesh['x'=4,'core'=2,'ka'=64] {'x','core'}, dimensions={0} | all-to-all | bytes 131072 | tf_op jit(solution)/shard_map/all_to_all | solution.py:287
  116.9 0.6 shard_map.88
Async XLA Ops:
  3.3 9.0 %collective-permute-start = (bf16[1040,128]{1,0:T(8,128)(2,1)S(1)}, bf16[1040,128]{1,0:T(8,128)(2,1)S(1)}, u32[]{:S(2)}, u32[]{:S(2)}) collective-permute-start(bf16[1040,128]{1,0:T(8,128)(2,1)S(1)} %get-tuple-element.13.w0), channel_id=1, source_target_pairs={{0,128},{64,192},{128,256},{192,320},{256,384},{320,448},{384,0},{... | collective-permute-start | bytes 798728 | tf_op jit(solution)/shard_map/ppermute | solution.py:271
  7.2 48.6 %collective-permute-start.2 = (bf16[1040,128]{1,0:T(8,128)(2,1)S(1)}, bf16[1040,128]{1,0:T(8,128)(2,1)S(1)}, u32[]{:S(2)}, u32[]{:S(2)}) collective-permute-start(bf16[1040,128]{1,0:T(8,128)(2,1)S(1)} %get-tuple-element.13.w0), channel_id=1, source_target_pairs={{128,0},{192,64},{256,128},{320,192},{384,256},{448,320},{129,1},{... | collective-permute-start | bytes 798728 | tf_op jit(solution)/shard_map/ppermute | solution.py:272
  12.3 43.5 %collective-permute-start.1 = (bf16[1040,128]{1,0:T(8,128)(2,1)S(1)}, bf16[1040,128]{1,0:T(8,128)(2,1)S(1)}, u32[]{:S(2)}, u32[]{:S(2)}) collective-permute-start(bf16[1040,128]{1,0:T(8,128)(2,1)S(1)} %collective-permute-done.w1), channel_id=1, source_target_pairs={{0,128},{64,192},{128,256},{192,320},{384,0},{448,64},{1,129},{65,... | collective-permute-start | bytes 798728 | tf_op jit(solution)/shard_map/ppermute | solution.py:273
